TPU v7x, 256 devices: a whole 4x4x8 slice. The times are simulated.
256 devices in a mesh: expert: 16 (over x, y), dp: 16 (over z, core).
Axes of the slice: x: 4, y: 4, z: 8, core: 2. Of those that a mesh axis runs over, the one named last changes fastest.
Arguments:
- tokens: bfloat16 [2, 32768, 1280], P(None, ('expert', 'dp')), may hold values from -6 to 6
- modality: int32 [2, 32768], P(None, ('expert', 'dp')), may hold values from 0 to 1, as said below
- routes: int32 [2, 32768, 1], P(None, ('expert', 'dp')), may hold values from 0 to 15; in each aligned block of 128 rows (0 to 127, 128 to 255, ..., all dimensions but the last counted through in order) at most 16 rows name the same one
- router: bfloat16 [1280, 16], replicated, may hold values from -0.15625 to 0.15625
- w_in: bfloat16 [16, 1280, 5120], P('expert', 'dp'), may hold values from -0.15625 to 0.15625
- w_out: bfloat16 [16, 5120, 1280], P('expert', 'dp'), may hold values from -0.078125 to 0.078125
Outputs:
- mixed: bfloat16 [2, 32768, 1280], P(None, ('expert', 'dp'))
- load: float32 [2, 2, 16], replicated
Inputs may be any that keep to these rules, and one draw needn't show every extreme that they name: `routes`: among the 128 tokens of one micro-batch on one device (aligned blocks of 128 rows), at most 16 are routed to any one expert. `modality`: in every aligned block of 128 tokens of a micro-batch, the number of text tokens lies between 32 and 96.
All inputs are finite; a program needn't handle non-finite values.
Results may differ from a plain program's by a relative error of at most 0.0057.
Values may be sent and summed in bfloat16 or wider, within the bound.
No kernel may reach another device: no remote copies, remote signals or barrier semaphores. Data moves between devices by JAX's collectives and lax.ppermute only.
A program may use at most 192 MiB of HBM per device.

v0:
```python
import jax
import jax.numpy as jnp
from jax import lax
from jax.sharding import Mesh
from jax.sharding import PartitionSpec as P

EXPERT = ("expert_0", "expert_1")
DP = ("dp_0", "dp_1")
EXPERT_DP = ("expert_0", "expert_1", "dp_0", "dp_1")


def over_axes(shard, axes):
    for axis in axes:
        shard = lax.psum(shard, axis)
    return shard


def on_device(tokens, modality, routes, router, w_in, w_out):
    micro_count, tok_count, model_width = tokens.shape
    experts = router.shape[1]
    capacity = 2 * tok_count // experts
    logits = jnp.einsum("mtd,de->mte", tokens, router, preferred_element_type=jnp.float32)
    onehot = (routes == jnp.arange(experts, dtype=jnp.int32)[None, None, :]).astype(jnp.float32)
    gating = jax.nn.sigmoid(jnp.sum(logits * onehot, axis=-1))
    running = jnp.cumsum(onehot, axis=1)
    slot_pos = jnp.sum((running - 1.0) * onehot, axis=-1)
    slot_hot = (
        slot_pos[:, :, None] == jnp.arange(capacity, dtype=jnp.float32)[None, None, :]
    ).astype(jnp.float32)
    placer = (onehot[:, :, :, None] * slot_hot[:, :, None, :]).reshape(
        micro_count, tok_count, experts * capacity
    )
    placer = placer.astype(jnp.bfloat16)
    buffer = jnp.einsum("mtk,mtd->mkd", placer, tokens, preferred_element_type=jnp.float32)
    buffer = buffer.astype(jnp.bfloat16).reshape(micro_count, experts, capacity, model_width)
    arrived = lax.all_to_all(buffer, EXPERT, split_axis=1, concat_axis=1, tiled=True)
    token_rows = arrived.reshape(-1, model_width)
    columns = token_rows
    pre_act = jnp.dot(
        columns, lax.all_gather(w_in, DP, axis=1, tiled=True)[0], preferred_element_type=jnp.float32
    )
    hidden = jax.nn.gelu(pre_act, approximate=True).astype(jnp.bfloat16)
    columns = hidden
    served = jnp.dot(
        columns,
        lax.all_gather(w_out, DP, axis=1, tiled=True)[0],
        preferred_element_type=jnp.float32,
    )
    served = served.astype(jnp.bfloat16).reshape(arrived.shape)
    returned = lax.all_to_all(served, EXPERT, split_axis=1, concat_axis=1, tiled=True)
    returned = returned.reshape(micro_count, experts * capacity, model_width)
    combined = jnp.einsum("mtk,mkd->mtd", placer, returned, preferred_element_type=jnp.float32)
    mixed = (combined * gating[:, :, None]).astype(jnp.bfloat16)
    exps = jnp.exp(logits)
    router_probs = exps / jnp.sum(exps, axis=-1, keepdims=True)
    modal_hot = (modality[:, :, None] == jnp.arange(2, dtype=jnp.int32)[None, None, :]).astype(
        jnp.float32
    )
    counts = jnp.einsum("mtk,mte->ke", modal_hot, onehot, precision=lax.Precision.HIGHEST)
    prob_sums = jnp.einsum("mtk,mte->ke", modal_hot, router_probs, precision=lax.Precision.HIGHEST)
    modal_counts = jnp.sum(modal_hot, axis=(0, 1))
    counts, prob_sums, modal_counts = (
        over_axes(counts, EXPERT_DP),
        over_axes(prob_sums, EXPERT_DP),
        over_axes(modal_counts, EXPERT_DP),
    )
    load = jnp.stack(
        [experts * counts / modal_counts[:, None], experts * prob_sums / modal_counts[:, None]]
    )
    return (mixed, load)


def solution(mesh):
    torus = Mesh(mesh.devices.reshape(4, 4, 8, 2), ("expert_0", "expert_1", "dp_0", "dp_1"))
    in_specs = (
        P(None, EXPERT_DP, None),
        P(None, EXPERT_DP),
        P(None, EXPERT_DP, None),
        P(),
        P(EXPERT, DP, None),
        P(EXPERT, DP, None),
    )
    out_specs = (P(None, EXPERT_DP, None), P())
    return jax.shard_map(
        on_device, mesh=torus, in_specs=in_specs, out_specs=out_specs, check_vma=False
    )
```

profile of v0, /device:TPU:1, one launch (start us, length us, event | category | flops | bytes accessed | tf_op | source)
XLA Modules:
  0.0 258.7 jit_solution(4837752513307506845)
XLA Ops:
  7.2 0.0 copy-start
  7.2 0.0 all-gather.5.cloned.1.call-start
  7.2 0.7 all-gather.5.cloned.1.call-update
  7.9 0.0 all-gather.3.cloned.1.call-start
  8.0 0.7 all-gather.3.cloned.1.call-update
  8.7 0.7 fusion.30
  9.3 0.1 copy.21
  9.5 0.2 reduce_window_sum.11
  9.6 0.1 copy.22
  9.7 0.8 fusion.29
  10.5 0.5 convolution_convert_fusion
  11.0 0.1 copy.23
  11.1 26.3 %all_to_all.10 = bf16[2,16,16,1280]{3,2,0,1:T(8,128)(2,1)S(1)} all-to-all(bf16[2,16,16,1280]{3,2,0,1:T(8,128)(2,1)S(1)} %copy.23), channel_id=1, replica_groups=mesh['expert_0'=4,'expert_1'=4,'dp_0'=8,'dp_1'=2] {'expert_0','expert_1'}, dimensions={1} | all-to-all | bytes 2621440 | tf_op jit(solution)/shard_map/all_to_all | solution.py:36
  37.5 0.1 copy.24
  37.6 54.6 %all-gather.5.cloned.1.call-done = bf16[1,5120,1280]{2,1,0:T(8,128)(2,1)} async-done(((bf16[1,320,1280]{2,1,0:T(8,128)(2,1)}), bf16[1,5120,1280]{2,1,0:T(8,128)(2,1)}) %all-gather.5.cloned.1.call-update) | async-done | bytes 13107216 | tf_op jit(solution)/shard_map/all_gather | solution.py:46
  92.1 78.5 %all-gather.3.cloned.1.call-done = bf16[1,1280,5120]{2,1,0:T(8,128)(2,1)} async-done(((bf16[1,80,5120]{2,1,0:T(8,128)(2,1)}), bf16[1,1280,5120]{2,1,0:T(8,128)(2,1)}) %all-gather.3.cloned.1.call-update) | async-done | bytes 13107216 | tf_op jit(solution)/shard_map/all_gather | solution.py:40
  170.6 22.4 %fusion.20 = bf16[512,1280]{1,0:T(8,128)(2,1)S(1)} fusion(bf16[1,5120,1280]{2,1,0:T(8,128)(2,1)} %all-gather.5.cloned.1.call-done, bf16[512,1280]{1,0:T(8,128)(2,1)S(1)} %bitcast.41, bf16[1,1280,5120]{2,1,0:T(8,128)(2,1)} %all-gather.3.cloned.1.call-done), kind=kOutput, calls=%fused_computation.17 | convolution fusion | flops 13446021120 | bytes 28835840 | tf_op jit(solution)/shard_map/dot_general | solution.py:44
  193.0 0.0 copy-start.3
  193.0 1.2 copy.25
  194.2 6.5 %all-to-all-start.1 = ((bf16[2,16,16,1280]{3,2,0,1:T(8,128)(2,1)}), bf16[2,16,16,1280]{3,2,0,1:T(8,128)(2,1)S(1)}, u32[]{:S(2)}, u32[]{:S(2)}) async-start(bf16[2,16,16,1280]{3,2,0,1:T(8,128)(2,1)} %copy.25), calls=%async_computation.1 | async-start | bytes 2621440 | tf_op jit(solution)/shard_map/all_to_all | solution.py:50
  200.8 0.1 convert_reduce_fusion
  200.9 0.1 convolution_bitcast_fusion.1
  201.0 0.3 exponential_reduce_fusion
  201.4 0.1 convolution_bitcast_fusion
  201.5 18.4 %all-reduce.2 = (f32[2,16]{1,0:T(2,128)S(1)}, f32[2]{0:T(128)S(1)}, f32[2,16]{1,0:T(2,128)S(1)}) all-reduce(f32[2,16]{1,0:T(2,128)S(1)} %convolution_bitcast_fusion, f32[2]{0:T(128)S(1)} %convert_reduce_fusion, f32[2,16]{1,0:T(2,128)S(1)} %convolution_bitcast_fusion.1), channel_id=1, replica_groups=mesh['expert_0'=4,'expert_1'=4,'dp_0'=8,'dp_1'=2] {'expert_0'}, use_global_device_ids=true, to_apply=%region_13.14 | all-reduce | flops 66 | bytes 528 | tf_op jit(solution)/shard_map/psum | solution.py:14
  219.9 8.1 %all-reduce.1 = (f32[2,16]{1,0:T(2,128)S(1)}, f32[2]{0:T(128)S(1)}, f32[2,16]{1,0:T(2,128)S(1)}) all-reduce(f32[2,16]{1,0:T(2,128)S(1)} %get-tuple-element.10, f32[2]{0:T(128)S(1)} %get-tuple-element.11, f32[2,16]{1,0:T(2,128)S(1)} %get-tuple-element.12), channel_id=1, replica_groups=mesh['expert_0'=4,'expert_1'=4,'dp_0'=8,'dp_1'=2] {'expert_1'}, use_global_device_ids=true, to_apply=%region_14.15 | all-reduce | flops 66 | bytes 528 | tf_op jit(solution)/shard_map/psum | solution.py:14
  227.9 11.8 %all-reduce = (f32[2,16]{1,0:T(2,128)S(1)}, f32[2]{0:T(128)S(1)}, f32[2,16]{1,0:T(2,128)S(1)}) all-reduce(f32[2,16]{1,0:T(2,128)S(1)} %get-tuple-element.7, f32[2]{0:T(128)S(1)} %get-tuple-element.8, f32[2,16]{1,0:T(2,128)S(1)} %get-tuple-element.9), channel_id=1, replica_groups=mesh['expert_0'=4,'expert_1'=4,'dp_0'=8,'dp_1'=2] {'dp_0'}, use_global_device_ids=true, to_apply=%region_15.16 | all-reduce | flops 66 | bytes 528 | tf_op jit(solution)/shard_map/psum | solution.py:14
  239.7 10.2 %all-reduce.3 = (f32[2,16]{1,0:T(2,128)S(1)}, f32[2]{0:T(128)S(1)}, f32[2,16]{1,0:T(2,128)S(1)}) all-reduce(f32[2,16]{1,0:T(2,128)S(1)} %get-tuple-element.4, f32[2]{0:T(128)S(1)} %get-tuple-element.5, f32[2,16]{1,0:T(2,128)S(1)} %get-tuple-element.6), channel_id=1, replica_groups=mesh['expert_0'=4,'expert_1'=4,'dp_0'=8,'dp_1'=2] {'dp_1'}, use_global_device_ids=true, to_apply=%region_16.17 | all-reduce | flops 66 | bytes 528 | tf_op jit(solution)/shard_map/psum | solution.py:14
  249.9 0.1 divide_bitcast_fusion.1
  249.9 0.6 pad_maximum_fusion
  250.5 0.1 copy.26
  250.6 1.2 fusion.25
  (9 shorter events, 0.1 us)
Async XLA Ops:
  7.2 3.3 %copy-start = (bf16[2,128,1280]{2,1,0:T(8,128)(2,1)S(1)}, bf16[2,128,1280]{2,1,0:T(8,128)(2,1)}, u32[]{:S(2)}) copy-start(bf16[2,128,1280]{2,1,0:T(8,128)(2,1)} %param.6) | copy-start | bytes 1966084
  7.2 84.9 %all-gather.5.cloned.1.call-start = ((), (), s32[]{:S(2)}) async-start(), calls=%async_computation.3 | async-start | bytes 13926400 | tf_op jit(solution)/shard_map/all_gather | solution.py:46
  7.9 162.7 %all-gather.3.cloned.1.call-start = ((), (), s32[]{:S(2)}) async-start(), calls=%async_computation.2 | async-start | bytes 13926400 | tf_op jit(solution)/shard_map/all_gather | solution.py:40
  193.0 7.8 %copy-start.3 = (s32[2,128]{1,0:T(2,128)S(1)}, s32[2,128]{1,0:T(2,128)}, u32[]{:S(2)}) copy-start(s32[2,128]{1,0:T(2,128)} %param.7) | copy-start | bytes 3076
  193.0 7.9 %copy-start.2 = (s32[2,128,1]{1,2,0:T(1,128)S(1)}, s32[2,128,1]{1,2,0:T(1,128)}, u32[]{:S(2)}) copy-start(s32[2,128,1]{1,2,0:T(1,128)} %param.8) | copy-start | bytes 3076
  193.0 8.0 %copy-start.1 = (bf16[1280,16]{0,1:T(8,128)(2,1)S(1)}, bf16[1280,16]{0,1:T(8,128)(2,1)}, u32[]{:S(2)}) copy-start(bf16[1280,16]{0,1:T(8,128)(2,1)} %param.9) | copy-start | bytes 122884
  194.2 56.3 %all-to-all-start.1 = ((bf16[2,16,16,1280]{3,2,0,1:T(8,128)(2,1)}), bf16[2,16,16,1280]{3,2,0,1:T(8,128)(2,1)S(1)}, u32[]{:S(2)}, u32[]{:S(2)}) async-start(bf16[2,16,16,1280]{3,2,0,1:T(8,128)(2,1)} %copy.25), calls=%async_computation.1 | async-start | bytes 2621440 | tf_op jit(solution)/shard_map/all_to_all | solution.py:50
Sparse Core Ops, SparseCore 0:
  9.8 82.2 all-gather.4
  93.9 76.5 all-gather.2
where the time goes:
time: 259 us
  waiting for transfers between devices  134 us (52%)
  blocking collectives  74.7 us (29%)
  matrix products  24.7 us (10%)
  between operations  14.2 us (5%)
  starting transfers between devices  6.6 us (3%)
    all_gather x1, waiting for transfers between devices, on_device(): lax.all_gather(w_in, DP, axis=1, tiled=True)[0]  78.5 us
    all_gather x1, waiting for transfers between devices, on_device(): lax.all_gather(w_out, DP, axis=1, tiled=True)[0]  54.6 us
    psum x4, blocking collectives, over_axes(): shard = lax.psum(shard, axis)  48.4 us
    all_to_all x1, blocking collectives, on_device(): lax.all_to_all(buffer, EXPERT, split_axis=1, concat_axis=1, tiled=True)  26.3 us
    dot_general x1, matrix products, on_device(): jnp.dot(columns, lax.all_gather(w_out, DP, axis=1, tiled=True)[0], prefer...  22.4 us
    all_to_all x1, starting transfers between devices, on_device(): lax.all_to_all(served, EXPERT, split_axis=1, concat_axis=1, tiled=True)  6.52 us
  transfers between devices with their start and end apart: 3, of which 2 were waited for; matrix products, arithmetic and copies ran while one was open for 2% of the time, Pallas kernels for 0%

commit v1 on v0

--- a/solution.py
+++ b/solution.py
@@ -33,7 +33,10 @@
     placer = placer.astype(jnp.bfloat16)
     buffer = jnp.einsum("mtk,mtd->mkd", placer, tokens, preferred_element_type=jnp.float32)
     buffer = buffer.astype(jnp.bfloat16).reshape(micro_count, experts, capacity, model_width)
-    arrived = lax.all_to_all(buffer, EXPERT, split_axis=1, concat_axis=1, tiled=True)
+    raw_out = jnp.split(buffer, lax.axis_size(EXPERT), 1)
+    tmp = jnp.stack(raw_out, axis=0)
+    w2 = lax.all_to_all(tmp, EXPERT, 0, 0)
+    arrived = jnp.concatenate(w2, 1)
     token_rows = arrived.reshape(-1, model_width)
     columns = token_rows
     pre_act = jnp.dot(

time: 259 us -> 259 us (level)
    all_gather x1, waiting for transfers between devices: 54.6 us -> 78.5 us  [on_device(): lax.all_gather(w_out, DP, axis=1, tiled=True)[0]]
    all_gather x1, waiting for transfers between devices: 78.5 us -> 55.8 us  [on_device(): lax.all_gather(w_in, DP, axis=1, tiled=True)[0]]
  transfers between devices with their start and end apart: 3 -> 3, of which waited for: 2 -> 2; matrix products, arithmetic and copies ran while one was open for 2% -> 1% of each run, Pallas kernels for 0% -> 0%
where the time goes in v1:
time: 259 us
  waiting for transfers between devices  136 us (53%)
  blocking collectives  74.7 us (29%)
  matrix products  24.9 us (10%)
  between operations  14.3 us (6%)
  starting transfers between devices  6.73 us (3%)
    all_gather x1, waiting for transfers between devices, on_device(): lax.all_gather(w_out, DP, axis=1, tiled=True)[0]  78.5 us
    all_gather x1, waiting for transfers between devices, on_device(): lax.all_gather(w_in, DP, axis=1, tiled=True)[0]  55.8 us
    psum x4, blocking collectives, over_axes(): shard = lax.psum(shard, axis)  48.4 us
    all_to_all x1, blocking collectives, on_device(): w2 = lax.all_to_all(tmp, EXPERT, 0, 0)  26.3 us
    dot_general x1, matrix products, on_device(): jnp.dot(columns, lax.all_gather(w_out, DP, axis=1, tiled=True)[0], prefer...  22.6 us
    all_to_all x1, starting transfers between devices, on_device(): lax.all_to_all(served, EXPERT, split_axis=1, concat_axis=1, tiled=True)  6.66 us
  transfers between devices with their start and end apart: 3, of which 2 were waited for; matrix products, arithmetic and copies ran while one was open for 1% of the time, Pallas kernels for 0%

profile of v1, /device:TPU:1, one launch (start us, length us, event | category | flops | bytes accessed | tf_op | source)
XLA Modules:
  0.0 259.0 jit_solution(8694648168887669077)
XLA Ops:
  7.2 0.0 copy-start
  7.2 0.0 copy-start.2
  7.2 0.0 all-gather.3.cloned.1.call-start
  7.2 0.7 all-gather.3.cloned.1.call-update
  7.9 0.0 all-gather.5.cloned.1.call-start
  8.0 0.7 all-gather.5.cloned.1.call-update
  8.7 0.1 copy.46
  8.8 0.2 reduce_window_sum.11
  9.0 0.1 copy.47
  9.0 0.1 fusion.45
  9.2 0.5 convolution_convert_fusion
  9.9 26.3 %all_to_all.10 = bf16[16,2,1,16,1280]{4,3,1,2,0:T(8,128)(2,1)S(1)} all-to-all(bf16[16,2,1,16,1280]{4,3,1,2,0:T(8,128)(2,1)S(1)} %fusion.26), channel_id=1, replica_groups=mesh['expert_0'=4,'expert_1'=4,'dp_0'=8,'dp_1'=2] {'expert_0','expert_1'}, dimensions={0} | all-to-all | bytes 2621440 | tf_op jit(solution)/shard_map/all_to_all | solution.py:38
  36.2 0.1 copy.64
  36.3 55.8 %all-gather.3.cloned.1.call-done = bf16[1,1280,5120]{2,1,0:T(8,128)(2,1)} async-done(((bf16[1,80,5120]{2,1,0:T(8,128)(2,1)}), bf16[1,1280,5120]{2,1,0:T(8,128)(2,1)}) %all-gather.3.cloned.1.call-update) | async-done | bytes 13107216 | tf_op jit(solution)/shard_map/all_gather | solution.py:43
  92.1 78.5 %all-gather.5.cloned.1.call-done = bf16[1,5120,1280]{2,1,0:T(8,128)(2,1)} async-done(((bf16[1,320,1280]{2,1,0:T(8,128)(2,1)}), bf16[1,5120,1280]{2,1,0:T(8,128)(2,1)}) %all-gather.5.cloned.1.call-update) | async-done | bytes 13107216 | tf_op jit(solution)/shard_map/all_gather | solution.py:49
  170.6 22.6 %fusion.20 = bf16[512,1280]{1,0:T(8,128)(2,1)S(1)} fusion(bf16[1,5120,1280]{2,1,0:T(8,128)(2,1)} %all-gather.5.cloned.1.call-done, bf16[512,1280]{1,0:T(8,128)(2,1)S(1)} %bitcast.154, bf16[1,1280,5120]{2,1,0:T(8,128)(2,1)} %all-gather.3.cloned.1.call-done), kind=kOutput, calls=%fused_computation.17 | convolution fusion | flops 13446021120 | bytes 28835840 | tf_op jit(solution)/shard_map/dot_general | solution.py:47
  193.2 1.2 copy.65
  194.4 6.7 %all-to-all-start.1 = ((bf16[2,16,16,1280]{3,2,0,1:T(8,128)(2,1)}), bf16[2,16,16,1280]{3,2,0,1:T(8,128)(2,1)S(1)}, u32[]{:S(2)}, u32[]{:S(2)}) async-start(bf16[2,16,16,1280]{3,2,0,1:T(8,128)(2,1)} %copy.65), calls=%async_computation.1 | async-start | bytes 2621440 | tf_op jit(solution)/shard_map/all_to_all | solution.py:53
  201.1 0.0 copy-done.3
  201.1 0.1 convert_reduce_fusion
  201.2 0.1 convolution_bitcast_fusion.1
  201.3 0.3 exponential_reduce_fusion
  201.7 0.1 convolution_bitcast_fusion
  201.8 18.4 %all-reduce.2 = (f32[2,16]{1,0:T(2,128)S(1)}, f32[2]{0:T(128)S(1)}, f32[2,16]{1,0:T(2,128)S(1)}) all-reduce(f32[2,16]{1,0:T(2,128)S(1)} %convolution_bitcast_fusion, f32[2]{0:T(128)S(1)} %convert_reduce_fusion, f32[2,16]{1,0:T(2,128)S(1)} %convolution_bitcast_fusion.1), channel_id=1, replica_groups=mesh['expert_0'=4,'expert_1'=4,'dp_0'=8,'dp_1'=2] {'expert_0'}, use_global_device_ids=true, to_apply=%region_13.14 | all-reduce | flops 66 | bytes 528 | tf_op jit(solution)/shard_map/psum | solution.py:14
  220.2 8.1 %all-reduce.1 = (f32[2,16]{1,0:T(2,128)S(1)}, f32[2]{0:T(128)S(1)}, f32[2,16]{1,0:T(2,128)S(1)}) all-reduce(f32[2,16]{1,0:T(2,128)S(1)} %get-tuple-element.10, f32[2]{0:T(128)S(1)} %get-tuple-element.11, f32[2,16]{1,0:T(2,128)S(1)} %get-tuple-element.12), channel_id=1, replica_groups=mesh['expert_0'=4,'expert_1'=4,'dp_0'=8,'dp_1'=2] {'expert_1'}, use_global_device_ids=true, to_apply=%region_14.15 | all-reduce | flops 66 | bytes 528 | tf_op jit(solution)/shard_map/psum | solution.py:14
  228.2 11.8 %all-reduce = (f32[2,16]{1,0:T(2,128)S(1)}, f32[2]{0:T(128)S(1)}, f32[2,16]{1,0:T(2,128)S(1)}) all-reduce(f32[2,16]{1,0:T(2,128)S(1)} %get-tuple-element.7, f32[2]{0:T(128)S(1)} %get-tuple-element.8, f32[2,16]{1,0:T(2,128)S(1)} %get-tuple-element.9), channel_id=1, replica_groups=mesh['expert_0'=4,'expert_1'=4,'dp_0'=8,'dp_1'=2] {'dp_0'}, use_global_device_ids=true, to_apply=%region_15.16 | all-reduce | flops 66 | bytes 528 | tf_op jit(solution)/shard_map/psum | solution.py:14
  240.0 10.2 %all-reduce.3 = (f32[2,16]{1,0:T(2,128)S(1)}, f32[2]{0:T(128)S(1)}, f32[2,16]{1,0:T(2,128)S(1)}) all-reduce(f32[2,16]{1,0:T(2,128)S(1)} %get-tuple-element.4, f32[2]{0:T(128)S(1)} %get-tuple-element.5, f32[2,16]{1,0:T(2,128)S(1)} %get-tuple-element.6), channel_id=1, replica_groups=mesh['expert_0'=4,'expert_1'=4,'dp_0'=8,'dp_1'=2] {'dp_1'}, use_global_device_ids=true, to_apply=%region_16.17 | all-reduce | flops 66 | bytes 528 | tf_op jit(solution)/shard_map/psum | solution.py:14
  250.2 0.1 divide_bitcast_fusion.1
  250.2 0.6 pad_maximum_fusion
  250.8 0.0 all-to-all-done.1
  250.8 0.1 copy.66
  250.9 1.2 fusion.25
  (24 shorter events, 0.2 us)
Async XLA Ops:
  7.2 2.0 copy-start
  7.2 1.5 copy-start.2
  7.2 84.9 %all-gather.3.cloned.1.call-start = ((), (), s32[]{:S(2)}) async-start(), calls=%async_computation.2 | async-start | bytes 13926400 | tf_op jit(solution)/shard_map/all_gather | solution.py:43
  7.9 162.7 %all-gather.5.cloned.1.call-start = ((), (), s32[]{:S(2)}) async-start(), calls=%async_computation.3 | async-start | bytes 13926400 | tf_op jit(solution)/shard_map/all_gather | solution.py:49
  194.4 6.7 %copy-start.3 = (s32[2,128]{1,0:T(2,128)S(1)}, s32[2,128]{1,0:T(2,128)}, u32[]{:S(2)}) copy-start(s32[2,128]{1,0:T(2,128)} %param.7) | copy-start | bytes 3076
  194.4 6.9 %copy-start.1 = (bf16[1280,16]{0,1:T(8,128)(2,1)S(1)}, bf16[1280,16]{0,1:T(8,128)(2,1)}, u32[]{:S(2)}) copy-start(bf16[1280,16]{0,1:T(8,128)(2,1)} %param.9) | copy-start | bytes 122884
  194.4 56.4 %all-to-all-start.1 = ((bf16[2,16,16,1280]{3,2,0,1:T(8,128)(2,1)}), bf16[2,16,16,1280]{3,2,0,1:T(8,128)(2,1)S(1)}, u32[]{:S(2)}, u32[]{:S(2)}) async-start(bf16[2,16,16,1280]{3,2,0,1:T(8,128)(2,1)} %copy.65), calls=%async_computation.1 | async-start | bytes 2621440 | tf_op jit(solution)/shard_map/all_to_all | solution.py:53
Sparse Core Ops, SparseCore 0:
  9.8 82.2 all-gather.2
  94.0 76.5 all-gather.4
